TPU v7x, 32 devices: a whole 2x2x4 slice. The times are simulated.
32 devices in a mesh: channel: 4 (over z), tm: 4 (over y, core), beam: 2 (over x).
Axes of the slice: x: 2, y: 2, z: 4, core: 2. Of those that a mesh axis runs over, the one named last changes fastest.
Arguments:
- voltages: bfloat16 [2, 2048, 64, 1024], P(None, ('beam', 'channel'), None, 'tm'), may hold values from -6 to 6
- positions: int32 [2048], replicated, may hold values from 0 to 1023
- delays: int32 [32, 1024], P(None, 'channel'), may hold values from 0 to 63
Outputs:
- intensity: float32 [1024, 64, 1024], P(('beam', 'tm'), 'channel')
- dedispersed: float32 [1024, 32, 64], P(('beam', 'tm'), 'channel')
Inputs may be any that keep to these rules, and one draw needn't show every extreme that they name: `positions`: place on a grid of 4 cylinders by 256 places along each.
All inputs are finite; a program needn't handle non-finite values.
Results may differ from a plain program's by a relative error of at most 0.0071.
Values may be sent and summed in bfloat16 or wider, within the bound.
No kernel may reach another device: no remote copies, remote signals or barrier semaphores. Data moves between devices by JAX's collectives and lax.ppermute only.
A program may use at most 192 MiB of HBM per device.

v0:
```python
import math
import jax
import jax.numpy as jnp
from jax import lax
from jax.sharding import PartitionSpec as P

FEEDS = 2048
BEAMS = 1024
UPCH = 16
TAPS = 8
FINE = 1024
TWO_PI = 2.0 * math.pi
HIGHEST = lax.Precision.HIGHEST


def from_behind(value, axis, steps):
    count = lax.axis_size(axis)
    first, last = (max(0, -steps), min(count, count - steps))
    return lax.ppermute(value, axis, [(source, source + steps) for source in range(first, last)])


def window_table(tap_count, upch_factor):
    length = tap_count * upch_factor
    sample_index = jnp.arange(length).astype(jnp.float32)
    taper = jnp.sinc((sample_index - (length - 1) / 2.0) / upch_factor) * (
        0.5 - 0.5 * jnp.cos(TWO_PI * (sample_index + 0.5) / length)
    )
    taper = taper / jnp.sqrt(jnp.sum(taper * taper))
    return taper.reshape(tap_count, upch_factor)


def steering(positions, beam_start, item_count, places, feed_count):
    beam_ids = beam_start + jnp.arange(item_count)
    beam_east = beam_ids // places
    beam_north = beam_ids % places
    cylinder = positions // places
    along_row = positions % places
    coarse = beam_east[:, None] * cylinder[None, :] % 4
    north_turns = beam_north[:, None] * along_row[None, :] % places
    angles = TWO_PI * (coarse.astype(jnp.float32) / 4.0 + north_turns.astype(jnp.float32) / places)
    norm_scale = 1.0 / math.sqrt(feed_count)
    w_real = (jnp.cos(angles) * norm_scale).astype(jnp.bfloat16)
    w_imag = (-jnp.sin(angles) * norm_scale).astype(jnp.bfloat16)
    top_half = jnp.concatenate([w_real, -w_imag], axis=1)
    low_half = jnp.concatenate([w_imag, w_real], axis=1)
    return jnp.concatenate([top_half, low_half], axis=0)


def upchannel_matrix(upch_factor):
    sample_index = jnp.arange(128)
    frame_part = sample_index // upch_factor
    inner = sample_index % upch_factor
    same_frame = frame_part[:, None] == frame_part[None, :]
    angles = (inner[:, None] * inner[None, :] % upch_factor).astype(jnp.float32) * (
        TWO_PI / upch_factor
    )
    cos_part = jnp.where(same_frame, jnp.cos(angles), 0.0)
    sin_part = jnp.where(same_frame, -jnp.sin(angles), 0.0)
    top_half = jnp.concatenate([cos_part, sin_part], axis=1)
    low_half = jnp.concatenate([-sin_part, cos_part], axis=1)
    return jnp.concatenate([top_half, low_half], axis=0)


def per_device(voltages, positions, delays):
    places = BEAMS // 4
    by_channel = lax.all_to_all(voltages, "channel", split_axis=2, concat_axis=1, tiled=True)
    chan_count = by_channel.shape[2]
    sample_count = by_channel.shape[3]
    own_beams = BEAMS // lax.axis_size("beam")
    beam_start = lax.axis_index("beam") * own_beams
    feed_piece = lax.all_gather(by_channel, "beam", axis=1, tiled=True)
    piece_width = feed_piece.shape[1]
    weights = steering(positions, beam_start, own_beams, places, FEEDS)
    flat_piece = feed_piece.reshape(2 * piece_width, chan_count * sample_count)
    summed = jnp.dot(weights, flat_piece, preferred_element_type=jnp.float32)
    beams = summed.astype(jnp.bfloat16).reshape(2, own_beams, chan_count, sample_count)
    beam_count = beams.shape[1]
    chan_count = beams.shape[2]
    sample_count = beams.shape[3]
    rim_width = (TAPS - 1) * UPCH
    previous = from_behind(beams[:, :, :, sample_count - rim_width :], "tm", 1)
    extended = jnp.concatenate([previous, beams], axis=3)
    window = window_table(TAPS, UPCH)
    filtered = jnp.zeros(beams.shape, jnp.float32)
    for tap_index in range(TAPS):
        filtered = filtered + extended[
            :, :, :, tap_index * UPCH : tap_index * UPCH + sample_count
        ] * jnp.tile(window[tap_index], sample_count // UPCH)
    row_count = beam_count * chan_count
    tile_count = sample_count // 128
    halves = filtered.reshape(2, row_count, tile_count, 128)
    paired = jnp.concatenate([halves[0], halves[1]], axis=2)
    spectra = jnp.dot(paired, upchannel_matrix(UPCH), precision=HIGHEST)
    real_part = spectra[:, :, :128]
    imag_part = spectra[:, :, 128:]
    power_grid = (real_part * real_part + imag_part * imag_part).reshape(
        beam_count, chan_count, sample_count
    )
    intensity = lax.all_to_all(power_grid, "tm", split_axis=0, concat_axis=2, tiled=True)
    beam_local = intensity.shape[0]
    frame_count = intensity.shape[2] // UPCH
    frame_grid = intensity.reshape(beam_local, chan_count, frame_count, UPCH)
    centred = frame_grid - jnp.mean(frame_grid, axis=2, keepdims=True)
    frame_index = jnp.arange(frame_count)
    angles = (frame_index[:, None] * frame_index[None, :] % frame_count).astype(jnp.float32) * (
        TWO_PI / frame_count
    )
    forward = jnp.concatenate([jnp.cos(angles), -jnp.sin(angles)], axis=1)
    fine_local = chan_count * UPCH
    transformed = jnp.einsum("bcnk,nw->wbck", centred, forward, precision=HIGHEST)
    transformed = transformed.reshape(2, frame_count, beam_local, fine_local)
    trial_count = delays.shape[0]
    delay_cols = jnp.transpose(delays)
    bin_block = min(16, frame_count)

    def dedisperse(bin_start):
        frequency = bin_start + jnp.arange(bin_block)
        angle_grid = (frequency[:, None, None] * delay_cols[None, :, :] % frame_count).astype(
            jnp.float32
        ) * (TWO_PI / frame_count)
        cos_table = jnp.cos(angle_grid)
        sin_table = jnp.sin(angle_grid)
        table = jnp.concatenate(
            [
                jnp.concatenate([cos_table, -sin_table], axis=2),
                jnp.concatenate([sin_table, cos_table], axis=2),
            ],
            axis=1,
        )
        left_real = lax.dynamic_slice_in_dim(transformed[0], bin_start, bin_block, 0)
        left_imag = lax.dynamic_slice_in_dim(transformed[1], bin_start, bin_block, 0)
        left_side = jnp.concatenate([left_real, left_imag], axis=2)
        return jnp.einsum("vbk,vkd->vbd", left_side, table, precision=HIGHEST)

    trials = lax.map(dedisperse, jnp.arange(frame_count // bin_block) * bin_block)
    trials = trials.reshape(frame_count, beam_local, 2, trial_count)
    inverse = jnp.stack([jnp.cos(angles), -jnp.sin(angles)]) / (frame_count * math.sqrt(FINE))
    combined = lax.psum_scatter(trials, "channel", scatter_dimension=3, tiled=True)
    dedispersed = jnp.einsum("vbrd,rvn->bdn", combined, inverse, precision=HIGHEST)
    return (intensity, dedispersed)


def solution(mesh):
    return jax.shard_map(
        per_device,
        mesh=mesh,
        in_specs=(P(None, ("beam", "channel"), None, "tm"), P(), P(None, "channel")),
        out_specs=(P(("beam", "tm"), "channel", None), P(("beam", "tm"), "channel", None)),
        check_vma=False,
    )
```

profile of v0, /device:TPU:0, one launch (start us, length us, event | category | flops | bytes accessed | tf_op | source)
XLA Modules:
  0.0 1423.7 jit_solution(7562544665450734379)
XLA Ops:
  17.5 368.9 %all_to_all.36 = bf16[2,256,64,256]{3,1,0,2:T(8,128)(2,1)S(1)} all-to-all(bf16[2,256,64,256]{3,1,0,2:T(8,128)(2,1)S(1)} %copy.27), channel_id=1, replica_groups=mesh['channel'=4,'tm'=4,'beam'=2] {'channel'}, dimensions={2} | all-to-all | bytes 33554432 | tf_op jit(solution)/shard_map/all_to_all | solution.py:66
  386.4 11.2 copy.29
  398.4 19.3 %fusion.103 = bf16[512,2048]{1,0:T(8,128)(2,1)} fusion(s32[2048]{0:T(1024)S(1)} %get-tuple-element.115, s32[512]{0:T(512)S(1)} %get-tuple-element.127, s32[2048]{0:T(1024)S(1)} %get-tuple-element.114, s32[512]{0:T(512)S(1)} %get-tuple-element.128), kind=kLoop, calls=%fused_computation.179 | loop fusion | flops 37748736 | bytes 2117632 | tf_op jit(solution)/shard_map/neg | solution.py:44
  417.6 20.6 %multiply_convert_fusion = (bf16[512,2048]{1,0:T(8,128)(2,1)S(1)}, bf16[512,2048]{1,0:T(8,128)(2,1)}) fusion(s32[2048]{0:T(1024)S(1)} %get-tuple-element.115, s32[512]{0:T(512)S(1)} %get-tuple-element.127, s32[2048]{0:T(1024)S(1)} %get-tuple-element.114, s32[512]{0:T(512)S(1)} %get-tuple-element.128), kind=kLoop, calls=%fused_computation.85 | loop fusion | flops 36700160 | bytes 4214784 | tf_op jit(solution)/shard_map/convert_element_type | solution.py:43
  438.2 348.5 %all-gather.2.cloned.1.call-done = bf16[2,2048,16,256]{3,2,1,0:T(8,128)(2,1)} async-done(((bf16[2,1024,16,256]{3,2,1,0:T(8,128)(2,1)}), bf16[2,2048,16,256]{3,2,1,0:T(8,128)(2,1)}) %all-gather.2.cloned.1.call-update) | async-done | bytes 33554448 | tf_op jit(solution)/shard_map/all_gather | solution.py:71
  786.7 22.6 %copy.46 = bf16[512,8,16,256]{3,1,2,0:T(8,128)(2,1)} copy(bf16[512,8,16,256]{3,2,1,0:T(8,128)(2,1)} %bitcast.68) | data formatting | bytes 67108864
  809.3 44.5 %fusion.49 = bf16[1024,4096]{1,0:T(8,128)(2,1)} fusion(bf16[4096,4096]{1,0:T(8,128)(2,1)} %bitcast.69, bf16[512,2048]{1,0:T(8,128)(2,1)} %get-tuple-element.113, bf16[512,2048]{1,0:T(8,128)(2,1)S(1)} %get-tuple-element.112, bf16[512,2048]{1,0:T(8,128)(2,1)} %fusion.103), kind=kOutput, calls=%fused_computation.72 | convolution fusion | flops 34397487104 | bytes 48234496 | tf_op jit(solution)/shard_map/dot_general | solution.py:75
  891.9 62.1 %multiply_add_fusion = f32[2,512,16,256]{3,2,1,0:T(8,128)} fusion(bf16[2,512,16,256]{3,2,1,0:T(8,128)(2,1)} %bitcast.67, bf16[2,512,16,112]{3,2,1,0:T(8,128)(2,1)} %copy.31, f32[256]{0:T(256)S(1)} %mul.404, f32[256]{0:T(256)S(1)} %mul.401, f32[256]{0:T(256)S(1)} %mul.398, f32[256]{0:T(256)S(1)} %mul.395, f32[256]{0:T(256)S(1)} %mul.392, f32[256]{0:T(256)S(1)} %mul.389, ...), kind=kLoop, calls=%fused_computation.38 | loop fusion | flops 184549376 | bytes 28844032 | tf_op jit(solution)/shard_map/add | solution.py:86
  954.0 10.9 fusion.105
  965.0 10.8 squeeze.16
  982.9 10.8 squeeze.15
  1001.4 18.0 %fusion.28 = f32[8192,2,256]{2,0,1:T(8,128)} fusion(f32[8192,2,128]{2,0,1:T(8,128)S(1)} %copy-done, f32[8192,2,128]{2,0,1:T(8,128)} %copy.32, f32[128,128]{1,0:T(8,128)S(1)} %get-tuple-element.118, f32[128,128]{1,0:T(8,128)S(1)} %get-tuple-element.117, f32[128,128]{1,0:T(8,128)S(1)} %get-tuple-element.116), kind=kOutput, calls=%fused_computation.34 | convolution fusion | flops 12889292800 | bytes 33751040 | tf_op jit(solution)/shard_map/dot_general | solution.py:93
  1025.7 31.3 %copy.34 = f32[8192,2,128]{2,1,0:T(2,128)} copy(f32[8192,2,128]{2,0,1:T(8,128)S(1)} %fusion.38) | data formatting | bytes 16777216 | tf_op jit(solution)/shard_map/add | solution.py:96
  1057.0 11.5 reshape.221
  1068.5 39.4 %all-to-all-start.1 = ((f32[512,16,256]{2,1,0:T(8,128)}), f32[512,16,256]{2,1,0:T(8,128)}, u32[]{:S(2)}, u32[]{:S(2)}) async-start(f32[512,16,256]{2,1,0:T(8,128)} %reshape.221), calls=%async_computation.1 | async-start | bytes 16777216 | tf_op jit(solution)/shard_map/all_to_all | solution.py:99
  1108.0 93.0 %all-to-all-done.1 = f32[512,16,256]{2,1,0:T(8,128)} async-done(((f32[512,16,256]{2,1,0:T(8,128)}), f32[512,16,256]{2,1,0:T(8,128)}, u32[]{:S(2)}, u32[]{:S(2)}) %all-to-all-start.1) | async-done | bytes 8388640 | tf_op jit(solution)/shard_map/all_to_all | solution.py:99
  1234.8 16.1 %fusion.47 = f32[2,64,128,256]{3,1,2,0:T(8,128)S(1)} fusion(f32[2,64,64,1]{2,1,3,0:T(8,128)S(1)} %bitcast.74, f32[128,256,64]{1,2,0:T(8,128)} %copy.38), kind=kOutput, calls=%fused_computation.63 | convolution fusion | flops 3221225472 | bytes 25198592 | tf_op jit(solution)/shard_map/bcnk,nw->wbck/dot_general | solution.py:110
  1250.9 19.7 %copy.39 = f32[2,64,128,256]{3,2,1,0:T(8,128)} copy(f32[2,64,128,256]{3,1,2,0:T(8,128)S(1)} %fusion.47) | data formatting | bytes 33554432 | tf_op jit(solution)/shard_map/while | solution.py:135
  1270.6 96.8 %while.12 = (s32[]{:T(128)}, f32[4,16,128,64]{2,3,1,0:T(8,128)}, f32[2,64,128,256]{3,2,1,0:T(8,128)}, s32[4]{0:T(128)S(1)}, s32[256,32]{0,1:T(8,128)S(1)}, /*index=5*/s32[]{:T(128)}, s32[]{:T(128)}, s32[]{:T(128)}) while((s32[]{:T(128)}, f32[4,16,128,64]{2,3,1,0:T(8,128)}, f32[2,64,128,256]{3,2,1,0:T(8,128)}, s32[4]{0:T(128)S(1)}, ...), condition=%wide.region_3.4_spmd, body=%wide.region_2.3_spmd.sunk | while | flops 809893888 | bytes 49840404 | solution.py:135
  1273.9 11.0 fusion.118
  1298.1 11.0 fusion.118
  1322.3 11.0 fusion.118
  1346.5 11.0 fusion.118
  1380.6 33.9 %reduce-scatter.2.cloned.1.call-done = f32[64,128,2,8]{1,0,2,3:T(8,128)} async-done(((f32[64,128,2,32]{1,0,2,3:T(8,128)}), f32[64,128,2,8]{1,0,2,3:T(8,128)}) %reduce-scatter.2.cloned.1.call-update) | async-done | bytes 524304 | tf_op jit(solution)/shard_map/reduce_scatter | solution.py:138
  (77 shorter events, 164.8 us)
Async XLA Ops:
  7.2 779.5 %all-gather.2.cloned.1.call-start = ((), (), s32[]{:S(2)}) async-start(), calls=%async_computation.3 | async-start | bytes 50331648 | tf_op jit(solution)/shard_map/all_gather | solution.py:71
  397.7 0.7 copy-start.2
  876.2 7.9 collective-permute-start
  993.7 7.7 copy-start
  1068.5 132.6 %all-to-all-start.1 = ((f32[512,16,256]{2,1,0:T(8,128)}), f32[512,16,256]{2,1,0:T(8,128)}, u32[]{:S(2)}, u32[]{:S(2)}) async-start(f32[512,16,256]{2,1,0:T(8,128)} %reshape.221), calls=%async_computation.1 | async-start | bytes 16777216 | tf_op jit(solution)/shard_map/all_to_all | solution.py:99
  1107.8 306.6 %reduce-scatter.2.cloned.1.call-start = ((), (), s32[]{:S(2)}) async-start(), calls=%async_computation.4 | async-start | bytes 2621440 | tf_op jit(solution)/shard_map/reduce_scatter | solution.py:138
  1250.9 19.7 %copy-start.1 = (s32[32,256]{1,0:T(8,128)S(1)}, s32[32,256]{1,0:T(8,128)}, u32[]{:S(2)}) copy-start(s32[32,256]{1,0:T(8,128)} %param.7) | copy-start | bytes 98308
Sparse Core Ops, SparseCore 0:
  397.8 388.8 all-gather.1
  1371.7 42.6 reduce-scatter.1
where the time goes:
time: 1430 us; the launch traced here: 1420 us
  waiting for transfers between devices  477 us (33%)
  blocking collectives  369 us (26%)
  local copies, waits for them, and re-layouts  281 us (20%)
  other arithmetic  129 us (9%)
  matrix products  103 us (7%)
  starting transfers between devices  42.8 us (3%)
  between operations  15 us (1%)
    all_to_all x1, blocking collectives, per_device(): lax.all_to_all(voltages, 'channel', split_axis=2, concat_axis=1, tiled=True)  369 us
    all_gather x1, waiting for transfers between devices, per_device(): feed_piece = lax.all_gather(by_channel, 'beam', axis=1, tiled=True)  348 us
    all_to_all x1, waiting for transfers between devices, per_device(): lax.all_to_all(power_grid, 'tm', split_axis=0, concat_axis=2, tiled=True)  93 us
    add x1, other arithmetic, per_device(): filtered + extended[:, :, :, tap_index * UPCH:tap_index * UPCH + sample_c...  62.1 us
    unnamed x11, local copies, waits for them, and re-layouts  59.5 us
    dot_general x1, matrix products, per_device(): summed = jnp.dot(weights, flat_piece, preferred_element_type=jnp.float32)  44.5 us
    slice x4, local copies, waits for them, and re-layouts, dedisperse(): transformed[0]  43.9 us
    all_to_all x1, starting transfers between devices, per_device(): lax.all_to_all(power_grid, 'tm', split_axis=0, concat_axis=2, tiled=True)  39.4 us
  transfers between devices with their start and end apart: 4, of which 4 were waited for; matrix products, arithmetic and copies ran while one was open for 4% of the time, Pallas kernels for 0%

commit v1 on v0

--- a/solution.py
+++ b/solution.py
@@ -68,7 +68,9 @@
     sample_count = by_channel.shape[3]
     own_beams = BEAMS // lax.axis_size("beam")
     beam_start = lax.axis_index("beam") * own_beams
-    feed_piece = lax.all_gather(by_channel, "beam", axis=1, tiled=True)
+    feed_piece = jnp.concatenate(
+        lax.all_to_all(jnp.stack([by_channel] * lax.axis_size("beam")), "beam", 0, 0), axis=1
+    )
     piece_width = feed_piece.shape[1]
     weights = steering(positions, beam_start, own_beams, places, FEEDS)
     flat_piece = feed_piece.reshape(2 * piece_width, chan_count * sample_count)

time: 1430 us -> 1460 us (1.021)
  waiting for transfers between devices: 477 us -> 450 us
  other arithmetic: 129 us -> 151 us
  local copies, waits for them, and re-layouts: 281 us -> 303 us
    all_gather x1 -> x0, waiting for transfers between devices: 348 us -> none  [per_device(): feed_piece = lax.all_gather(by_channel, 'beam', axis=1, tiled=True)]
    all_to_all x0 -> x1, waiting for transfers between devices: none -> 321 us  [per_device(): lax.all_to_all(jnp.stack([by_channel] * lax.axis_size('beam')), 'beam', 0...]
    reshape x0 -> x1, local copies, waits for them, and re-layouts: none -> 22.8 us  [per_device(): jnp.concatenate(lax.all_to_all(jnp.stack([by_channel] * lax.axis_size('be...]
    another operation x0 -> x1, other arithmetic: none -> 22.4 us  [per_device(): jnp.stack([by_channel] * lax.axis_size('beam'))]
  transfers between devices with their start and end apart: 4 -> 4, of which waited for: 4 -> 4; matrix products, arithmetic and copies ran while one was open for 4% -> 3% of each run, Pallas kernels for 0% -> 0%
where the time goes in v1:
time: 1460 us; the launch traced here: 1450 us
  waiting for transfers between devices  450 us (31%)
  blocking collectives  369 us (25%)
  local copies, waits for them, and re-layouts  303 us (21%)
  other arithmetic  151 us (10%)
  matrix products  103 us (7%)
  starting transfers between devices  55.8 us (4%)
  between operations  15.1 us (1%)
    all_to_all x1, blocking collectives, per_device(): lax.all_to_all(voltages, 'channel', split_axis=2, concat_axis=1, tiled=True)  369 us
    all_to_all x1, waiting for transfers between devices, per_device(): lax.all_to_all(jnp.stack([by_channel] * lax.axis_size('beam')), 'beam', 0...  321 us
    all_to_all x1, waiting for transfers between devices, per_device(): lax.all_to_all(power_grid, 'tm', split_axis=0, concat_axis=2, tiled=True)  93 us
    add x1, other arithmetic, per_device(): filtered + extended[:, :, :, tap_index * UPCH:tap_index * UPCH + sample_c...  62 us
    unnamed x11, local copies, waits for them, and re-layouts  58.8 us
    dot_general x1, matrix products, per_device(): summed = jnp.dot(weights, flat_piece, preferred_element_type=jnp.float32)  44.4 us
    slice x4, local copies, waits for them, and re-layouts, dedisperse(): transformed[0]  43.8 us
    all_to_all x1, starting transfers between devices, per_device(): lax.all_to_all(power_grid, 'tm', split_axis=0, concat_axis=2, tiled=True)  39.6 us
  transfers between devices with their start and end apart: 4, of which 4 were waited for; matrix products, arithmetic and copies ran while one was open for 3% of the time, Pallas kernels for 0%

profile of v1, /device:TPU:0, one launch (start us, length us, event | category | flops | bytes accessed | tf_op | source)
XLA Modules:
  0.0 1454.9 jit_solution(15545338272840736354)
XLA Ops:
  17.5 368.9 %all_to_all.38 = bf16[2,256,64,256]{3,1,0,2:T(8,128)(2,1)S(1)} all-to-all(bf16[2,256,64,256]{3,1,0,2:T(8,128)(2,1)S(1)} %copy.29), channel_id=1, replica_groups=mesh['channel'=4,'tm'=4,'beam'=2] {'channel'}, dimensions={2} | all-to-all | bytes 33554432 | tf_op jit(solution)/shard_map/all_to_all | solution.py:66
  386.4 11.2 copy.31
  397.6 22.4 %pad_maximum_fusion = bf16[2,2,1024,16,256]{4,3,2,1,0:T(8,128)(2,1)} fusion(bf16[1,2,1024,16,256]{4,3,2,1,0:T(8,128)(2,1)} %bitcast.66), kind=kLoop, calls=%fused_computation.28 | loop fusion | flops 16777216 | bytes 50331648 | tf_op jit(solution)/shard_map/stack | solution.py:72
  420.1 13.0 all-to-all-start.1
  433.1 19.3 %fusion.103 = bf16[512,2048]{1,0:T(8,128)(2,1)} fusion(s32[2048]{0:T(1024)S(1)} %get-tuple-element.115, s32[512]{0:T(512)S(1)} %get-tuple-element.127, s32[2048]{0:T(1024)S(1)} %get-tuple-element.114, s32[512]{0:T(512)S(1)} %get-tuple-element.128), kind=kLoop, calls=%fused_computation.180 | loop fusion | flops 37748736 | bytes 2117632 | tf_op jit(solution)/shard_map/neg | solution.py:44
  452.4 20.6 %multiply_convert_fusion = (bf16[512,2048]{1,0:T(8,128)(2,1)S(1)}, bf16[512,2048]{1,0:T(8,128)(2,1)}) fusion(s32[2048]{0:T(1024)S(1)} %get-tuple-element.115, s32[512]{0:T(512)S(1)} %get-tuple-element.127, s32[2048]{0:T(1024)S(1)} %get-tuple-element.114, s32[512]{0:T(512)S(1)} %get-tuple-element.128), kind=kLoop, calls=%fused_computation.86 | loop fusion | flops 36700160 | bytes 4214784 | tf_op jit(solution)/shard_map/convert_element_type | solution.py:43
  472.9 321.3 %all-to-all-done.1 = bf16[2,2,1024,16,256]{4,3,2,1,0:T(8,128)(2,1)} async-done(((bf16[2,2,1024,16,256]{4,3,2,1,0:T(8,128)(2,1)}), bf16[2,2,1024,16,256]{4,3,2,1,0:T(8,128)(2,1)}, u32[]{:S(2)}, u32[]{:S(2)}) %all-to-all-start.1) | async-done | bytes 33554464 | tf_op jit(solution)/shard_map/all_to_all | solution.py:72
  794.2 22.8 %copy.32 = bf16[2,2,1024,16,256]{4,3,2,1,0:T(8,128)(2,1)} copy(bf16[2,2,1024,16,256]{4,3,2,0,1:T(8,128)(2,1)} %bitcast.8) | data formatting | bytes 67108864 | tf_op jit(solution)/shard_map/reshape | solution.py:71
  817.1 22.6 %copy.49 = bf16[512,8,16,256]{3,1,2,0:T(8,128)(2,1)} copy(bf16[512,8,16,256]{3,2,1,0:T(8,128)(2,1)} %bitcast.62) | data formatting | bytes 67108864
  839.7 44.4 %fusion.49 = bf16[1024,4096]{1,0:T(8,128)(2,1)} fusion(bf16[4096,4096]{1,0:T(8,128)(2,1)} %bitcast.70, bf16[512,2048]{1,0:T(8,128)(2,1)} %get-tuple-element.113, bf16[512,2048]{1,0:T(8,128)(2,1)S(1)} %get-tuple-element.112, bf16[512,2048]{1,0:T(8,128)(2,1)} %fusion.103), kind=kOutput, calls=%fused_computation.73 | convolution fusion | flops 34397487104 | bytes 48234496 | tf_op jit(solution)/shard_map/dot_general | solution.py:77
  922.0 62.0 %multiply_add_fusion = f32[2,512,16,256]{3,2,1,0:T(8,128)} fusion(bf16[2,512,16,256]{3,2,1,0:T(8,128)(2,1)} %bitcast.69, bf16[2,512,16,112]{3,2,1,0:T(8,128)(2,1)} %copy.34, f32[256]{0:T(256)S(1)} %mul.404, f32[256]{0:T(256)S(1)} %mul.401, f32[256]{0:T(256)S(1)} %mul.398, f32[256]{0:T(256)S(1)} %mul.395, f32[256]{0:T(256)S(1)} %mul.392, f32[256]{0:T(256)S(1)} %mul.389, ...), kind=kLoop, calls=%fused_computation.39 | loop fusion | flops 184549376 | bytes 28844032 | tf_op jit(solution)/shard_map/add | solution.py:88
  1031.3 18.0 %fusion.28 = f32[8192,2,256]{2,0,1:T(8,128)} fusion(f32[8192,2,128]{2,0,1:T(8,128)S(1)} %copy-done, f32[8192,2,128]{2,0,1:T(8,128)} %copy.35, f32[128,128]{1,0:T(8,128)S(1)} %get-tuple-element.118, f32[128,128]{1,0:T(8,128)S(1)} %get-tuple-element.117, f32[128,128]{1,0:T(8,128)S(1)} %get-tuple-element.116), kind=kOutput, calls=%fused_computation.35 | convolution fusion | flops 12889292800 | bytes 33751040 | tf_op jit(solution)/shard_map/dot_general | solution.py:95
  1055.6 31.3 %copy.37 = f32[8192,2,128]{2,1,0:T(2,128)} copy(f32[8192,2,128]{2,0,1:T(8,128)S(1)} %fusion.38) | data formatting | bytes 16777216 | tf_op jit(solution)/shard_map/add | solution.py:98
  1086.8 11.5 reshape.222
  1098.3 39.6 %all-to-all-start.2 = ((f32[512,16,256]{2,1,0:T(8,128)}), f32[512,16,256]{2,1,0:T(8,128)}, u32[]{:S(2)}, u32[]{:S(2)}) async-start(f32[512,16,256]{2,1,0:T(8,128)} %reshape.222), calls=%async_computation.2 | async-start | bytes 16777216 | tf_op jit(solution)/shard_map/all_to_all | solution.py:101
  1138.2 93.0 %all-to-all-done.2 = f32[512,16,256]{2,1,0:T(8,128)} async-done(((f32[512,16,256]{2,1,0:T(8,128)}), f32[512,16,256]{2,1,0:T(8,128)}, u32[]{:S(2)}, u32[]{:S(2)}) %all-to-all-start.2) | async-done | bytes 8388640 | tf_op jit(solution)/shard_map/all_to_all | solution.py:101
  1264.8 16.1 %fusion.47 = f32[2,64,128,256]{3,1,2,0:T(8,128)S(1)} fusion(f32[2,64,64,1]{2,1,3,0:T(8,128)S(1)} %bitcast.75, f32[128,256,64]{1,2,0:T(8,128)} %copy.41), kind=kOutput, calls=%fused_computation.64 | convolution fusion | flops 3221225472 | bytes 25198592 | tf_op jit(solution)/shard_map/bcnk,nw->wbck/dot_general | solution.py:112
  1280.9 19.7 %copy.42 = f32[2,64,128,256]{3,2,1,0:T(8,128)} copy(f32[2,64,128,256]{3,1,2,0:T(8,128)S(1)} %fusion.47) | data formatting | bytes 33554432 | tf_op jit(solution)/shard_map/while | solution.py:137
  1300.6 98.0 %while.12 = (s32[]{:T(128)}, f32[4,16,128,64]{2,3,1,0:T(8,128)}, f32[2,64,128,256]{3,2,1,0:T(8,128)}, s32[4]{0:T(128)S(1)}, s32[256,32]{0,1:T(8,128)S(1)}, /*index=5*/s32[]{:T(128)}, s32[]{:T(128)}, s32[]{:T(128)}) while((s32[]{:T(128)}, f32[4,16,128,64]{2,3,1,0:T(8,128)}, f32[2,64,128,256]{3,2,1,0:T(8,128)}, s32[4]{0:T(128)S(1)}, ...), condition=%wide.region_3.4_spmd, body=%wide.region_2.3_spmd.sunk | while | flops 809893888 | bytes 49840404 | solution.py:137
  1304.0 11.0 fusion.118
  1328.5 11.0 fusion.118
  1353.0 11.0 fusion.118
  1377.5 11.0 fusion.118
  1411.8 33.9 %reduce-scatter.2.cloned.1.call-done = f32[64,128,2,8]{1,0,2,3:T(8,128)} async-done(((f32[64,128,2,32]{1,0,2,3:T(8,128)}), f32[64,128,2,8]{1,0,2,3:T(8,128)}) %reduce-scatter.2.cloned.1.call-update) | async-done | bytes 524304 | tf_op jit(solution)/shard_map/reduce_scatter | solution.py:140
  (78 shorter events, 196.6 us)
Async XLA Ops:
  420.0 13.0 copy-start.2
  420.1 374.2 %all-to-all-start.1 = ((bf16[2,2,1024,16,256]{4,3,2,1,0:T(8,128)(2,1)}), bf16[2,2,1024,16,256]{4,3,2,1,0:T(8,128)(2,1)}, u32[]{:S(2)}, u32[]{:S(2)}) async-start(bf16[2,2,1024,16,256]{4,3,2,1,0:T(8,128)(2,1)} %pad_maximum_fusion), calls=%async_computation.1 | async-start | bytes 67108864 | tf_op jit(solution)/shard_map/all_to_all | solution.py:72
  906.6 7.6 collective-permute-start
  1023.6 7.7 copy-start
  1098.3 132.8 %all-to-all-start.2 = ((f32[512,16,256]{2,1,0:T(8,128)}), f32[512,16,256]{2,1,0:T(8,128)}, u32[]{:S(2)}, u32[]{:S(2)}) async-start(f32[512,16,256]{2,1,0:T(8,128)} %reshape.222), calls=%async_computation.2 | async-start | bytes 16777216 | tf_op jit(solution)/shard_map/all_to_all | solution.py:101
  1138.0 307.7 %reduce-scatter.2.cloned.1.call-start = ((), (), s32[]{:S(2)}) async-start(), calls=%async_computation.4 | async-start | bytes 2621440 | tf_op jit(solution)/shard_map/reduce_scatter | solution.py:140
  1280.9 19.7 %copy-start.1 = (s32[32,256]{1,0:T(8,128)S(1)}, s32[32,256]{1,0:T(8,128)}, u32[]{:S(2)}) copy-start(s32[32,256]{1,0:T(8,128)} %param.7) | copy-start | bytes 98308
Sparse Core Ops, SparseCore 0:
  1402.9 42.6 reduce-scatter.1
